TPU v7x, 32 devices: a whole 2x2x4 slice. The times are simulated.
32 devices in a mesh: dp: 8 (over y, x, core), fsdp: 4 (over z).
Axes of the slice: x: 2, y: 2, z: 4, core: 2. Of those that a mesh axis runs over, the one named last changes fastest.
Arguments:
- tokens: bfloat16 [4096, 4096], P('dp'), may hold values from -6 to 6
- counts: int32 [8], P('dp'), may hold values from 256 to 512, as said below
- patch_index: int32 [4096], P('dp'), may hold values from 0 to 255
- clip_limit: float32 [], replicated, may hold values from 1024 to 8192
- norm_gain: float32 [4, 4096], replicated, may hold values from 0.25 to 1.75
- params: float32 [4, 4096, 4096], P(None, 'dp', 'fsdp'), may hold values from -0.09375 to 0.09375
- moments: float32 [4, 4096, 4096], P(None, 'dp', 'fsdp'), may hold values from -0.3 to 0.3
- seconds: float32 [4, 4096, 4096], P(None, 'dp', 'fsdp'), may hold values from 0.05 to 1
- gradients: float32 [4, 4096, 4096], P(None, 'dp', 'fsdp'), may hold values from -48 to 48
Outputs:
- params_new: float32 [4, 4096, 4096], P(None, 'dp', 'fsdp')
- moments_new: float32 [4, 4096, 4096], P(None, 'dp', 'fsdp')
- seconds_new: float32 [4, 4096, 4096], P(None, 'dp', 'fsdp')
- mixed: bfloat16 [4096, 4096], P('dp', 'fsdp')
Inputs may be any that keep to these rules, and one draw needn't show every extreme that they name: `counts`: at most 512, reached on some index of dp in every draw.
All inputs are finite; a program needn't handle non-finite values.
Results may differ from a plain program's by a relative error of at most 0.0095.
Values may be sent and summed in bfloat16 or wider, within the bound.
A program may use at most 192 MiB of HBM per device.

v0:
```python
import jax
import jax.numpy as jnp
from jax import lax
from jax.sharding import PartitionSpec as P

D = 4096
LAYERS = 4
GRID = 16
STEP = 40
beta_one = 0.9
beta_two = 0.95
adam_eps = 1e-08
learning_rate = 0.0024
weight_decay = 0.05
norm_eps = 1e-06


def position_code(patch_index):
    quarter = D // 4
    freqs = 1.0 / 10000.0 ** (jnp.arange(quarter, dtype=jnp.float32) / quarter)
    across = (patch_index // GRID).astype(jnp.float32)[:, None] * freqs[None, :]
    downward = (patch_index % GRID).astype(jnp.float32)[:, None] * freqs[None, :]
    return jnp.concatenate(
        [jnp.sin(across), jnp.cos(across), jnp.sin(downward), jnp.cos(downward)], axis=1
    )


def layer_norm(stream, gain_row):
    centre = jnp.mean(stream, axis=1, keepdims=True)
    shifted = stream - centre
    spread = jnp.mean(shifted * shifted, axis=1, keepdims=True)
    return (shifted * lax.rsqrt(spread + norm_eps) * gain_row[None, :]).astype(jnp.bfloat16)


def adam_update(params, moments, seconds, gradients, factor):
    clipped = gradients * factor
    moments_new = beta_one * moments + (1.0 - beta_one) * clipped
    seconds_new = beta_two * seconds + (1.0 - beta_two) * clipped * clipped
    direction = (
        moments_new
        / (1.0 - beta_one**STEP)
        / (jnp.sqrt(seconds_new / (1.0 - beta_two**STEP)) + adam_eps)
    )
    params_new = params - learning_rate * (direction + weight_decay * params)
    return (params_new, moments_new, seconds_new)


def advance(stream, branch, current, col_first, col_count):
    if current + 1 < LAYERS:
        widened = lax.all_gather(branch, "fsdp", axis=1, tiled=True)
        return stream + widened.astype(jnp.float32)
    return lax.dynamic_slice_in_dim(stream, col_first, col_count, 1) + branch.astype(jnp.float32)


def per_device(
    tokens, counts, patch_index, clip_limit, norm_gain, params, moments, seconds, gradients
):
    squares = lax.psum(jnp.sum(gradients * gradients), ("dp", "fsdp"))
    factor = jnp.minimum(1.0, clip_limit / (jnp.sqrt(squares) + 1e-06))
    params_new, moments_new, seconds_new = adam_update(params, moments, seconds, gradients, factor)
    weights = params_new.astype(jnp.bfloat16)
    tok_rows = tokens.shape[0]
    col_count = weights.shape[2]
    col_first = lax.axis_index("fsdp") * col_count
    valid = lax.broadcasted_iota(jnp.int32, (tok_rows, 1), 0) < counts[0]
    stream = jnp.where(valid, tokens.astype(jnp.float32) + position_code(patch_index), 0.0)
    gathered = lax.all_gather(weights, "dp", axis=1, tiled=True)
    for current in range(LAYERS):
        normed = layer_norm(stream, norm_gain[current])
        branch = jnp.dot(normed, gathered[current], preferred_element_type=jnp.float32).astype(
            jnp.bfloat16
        )
        stream = advance(stream, branch, current, col_first, col_count)
    mixed = jnp.where(valid, stream, 0.0).astype(jnp.bfloat16)
    return (params_new, moments_new, seconds_new, mixed)


def solution(mesh):
    in_specs = (
        P("dp", None),
        P("dp"),
        P("dp"),
        P(),
        P(),
        P(None, "dp", "fsdp"),
        P(None, "dp", "fsdp"),
        P(None, "dp", "fsdp"),
        P(None, "dp", "fsdp"),
    )
    out_specs = (
        P(None, "dp", "fsdp"),
        P(None, "dp", "fsdp"),
        P(None, "dp", "fsdp"),
        P("dp", "fsdp"),
    )
    return jax.shard_map(
        per_device, mesh=mesh, in_specs=in_specs, out_specs=out_specs, check_vma=False
    )
```

profile of v0, /device:TPU:0, one launch (start us, length us, event | category | flops | bytes accessed | tf_op | source)
XLA Modules:
  0.0 556.9 jit_solution(18285389573598532073)
XLA Ops:
  7.2 0.0 all-gather.5.cloned.1.call-start
  7.2 6.1 %multiply_reduce_fusion.4 = f32[]{:T(128)} fusion(f32[4,512,1024]{2,1,0:T(8,128)} %param.17), kind=kLoop, calls=%fused_computation.25 | loop fusion | flops 4194303 | bytes 8388612 | tf_op jit(solution)/shard_map/reduce_sum | solution.py:58
  14.0 42.2 %psum.7 = f32[]{:T(128)} all-reduce(f32[]{:T(128)} %multiply_reduce_fusion.4), channel_id=1, replica_groups=mesh['dp'=8,'fsdp'=4] {'dp','fsdp'}, use_global_device_ids=true, to_apply=%region_1.0 | all-reduce | flops 1 | bytes 8 | tf_op jit(solution)/shard_map/psum | solution.py:58
  57.0 20.8 %fusion.30 = (bf16[4,512,1024]{2,1,0:T(8,128)(2,1)}, f32[4,512,1024]{2,1,0:T(8,128)}, f32[4,512,1024]{2,1,0:T(8,128)}, f32[4,512,1024]{2,1,0:T(8,128)}) fusion(f32[4,512,1024]{2,1,0:T(8,128)} %param.14, f32[4,512,1024]{2,1,0:T(8,128)} %param.17, f32[]{:T(128)S(6)} %min.3, f32[4,512,1024]{2,1,0:T(8,128)} %param.15, f32[4,512,1024]{2,1,0:T(8,128)} %param.16), kind=kLoop, calls=%fused_computation.71 | loop fusion | flops 35651584 | bytes 62914564 | tf_op jit(solution)/shard_map/convert_element_type | solution.py:61
  77.8 0.0 all-gather.5.cloned.1.call-update
  77.8 0.2 all-gather.7.cloned.1.call-start
  78.0 0.0 copy-start.3
  78.9 14.7 %multiply_sine_fusion.1 = (f32[512,1024]{1,0:T(8,128)S(1)}, f32[512,1024]{1,0:T(8,128)S(1)}, f32[512,1024]{1,0:T(8,128)S(1)}, f32[512,1024]{1,0:T(8,128)S(1)}) fusion(f32[1024]{0:T(1024)S(1)} %negate_power_fusion, f32[512]{0:T(512)S(1)} %get-tuple-element.24, f32[512]{0:T(512)S(1)} %get-tuple-element.25), kind=kLoop, calls=%fused_computation.41 | loop fusion | flops 1048576 | bytes 8396800 | tf_op jit(solution)/shard_map/sin | solution.py:24
  93.7 1.7 fusion.28
  95.4 3.2 copy-done
  98.6 1.0 multiply_reduce_fusion.3
  99.6 139.0 %all-gather.5.cloned.1.call-done = bf16[4,4096,1024]{2,1,0:T(8,128)(2,1)} async-done(((bf16[4,512,1024]{2,1,0:T(8,128)(2,1)}), bf16[4,4096,1024]{2,1,0:T(8,128)(2,1)}) %all-gather.5.cloned.1.call-update) | async-done | bytes 33554448 | tf_op jit(solution)/shard_map/all_gather | solution.py:67
  238.6 11.3 %fusion.18 = bf16[512,1024]{1,0:T(8,128)(2,1)} fusion(bf16[4,4096,1024]{2,1,0:T(8,128)(2,1)} %all-gather.5.cloned.1.call-done, f32[512,4096]{1,0:T(8,128)} %copy-done, f32[4096]{0:T(1024)S(1)} %bitcast.33, f32[512]{0:T(512)S(1)} %add_rsqrt_fusion.3, f32[512]{0:T(512)S(1)} %broadcast_multiply_fusion.3), kind=kOutput, calls=%fused_computation.43 | convolution fusion | flops 4303880192 | bytes 17846272 | tf_op jit(solution)/shard_map/dot_general | solution.py:70
  249.9 0.0 all-gather.7.cloned.1.call-update
  249.9 0.0 all-gather.9.cloned.1.call-start
  250.0 80.8 %all-gather.7.cloned.1.call-done = bf16[512,4096]{1,0:T(8,128)(2,1)} async-done(((bf16[512,1024]{1,0:T(8,128)(2,1)}), bf16[512,4096]{1,0:T(8,128)(2,1)}) %all-gather.7.cloned.1.call-update) | async-done | bytes 4194320 | tf_op jit(solution)/shard_map/all_gather | solution.py:50
  330.8 5.6 %fusion.22 = f32[512]{0:T(512)S(1)} fusion(f32[512,4096]{1,0:T(8,128)} %copy-done, bf16[512,4096]{1,0:T(8,128)(2,1)} %all-gather.7.cloned.1.call-done), kind=kLoop, calls=%fused_computation.47 | loop fusion | flops 6290944 | bytes 12584960 | tf_op jit(solution)/shard_map/reduce_sum | solution.py:29
  336.4 0.1 copy-done.2
  336.6 5.2 multiply_reduce_fusion.2
  341.8 9.2 %fusion.19 = bf16[512,1024]{1,0:T(8,128)(2,1)} fusion(bf16[4,4096,1024]{2,1,0:T(8,128)(2,1)} %all-gather.5.cloned.1.call-done, f32[4096]{0:T(1024)S(1)} %bitcast.32, f32[512]{0:T(512)S(1)} %add_rsqrt_fusion.2, f32[512]{0:T(512)S(1)} %broadcast_multiply_fusion.2, f32[512,4096]{1,0:T(8,128)S(1)} %bitcast.29, bf16[512,4096]{1,0:T(8,128)(2,1)S(1)} %copy-done.2), kind=kOutput, calls=%fused_computation.44 | convolution fusion | flops 4308074496 | bytes 22040576 | tf_op jit(solution)/shard_map/dot_general | solution.py:70
  351.0 0.0 all-gather.9.cloned.1.call-update
  351.1 0.3 all-gather.11.cloned.1.call-start
  351.4 79.1 %all-gather.9.cloned.1.call-done = bf16[512,4096]{1,0:T(8,128)(2,1)} async-done(((bf16[512,1024]{1,0:T(8,128)(2,1)}), bf16[512,4096]{1,0:T(8,128)(2,1)}) %all-gather.9.cloned.1.call-update) | async-done | bytes 4194320 | tf_op jit(solution)/shard_map/all_gather | solution.py:50
  430.4 10.3 %fusion.27 = (f32[512]{0:T(512)S(1)}, f32[512,4096]{1,0:T(8,128)}) fusion(bf16[512,4096]{1,0:T(8,128)(2,1)} %all-gather.9.cloned.1.call-done, f32[512,4096]{1,0:T(8,128)} %copy-done, bf16[512,4096]{1,0:T(8,128)(2,1)} %all-gather.7.cloned.1.call-done), kind=kLoop, calls=%fused_computation.69 | loop fusion | flops 10485248 | bytes 25167872 | tf_op jit(solution)/shard_map/reduce_sum | solution.py:29
  440.8 4.5 multiply_reduce_fusion.1
  445.3 1.3 copy-done.1
  446.5 9.0 %fusion.20 = bf16[512,1024]{1,0:T(8,128)(2,1)} fusion(bf16[4,4096,1024]{2,1,0:T(8,128)(2,1)} %all-gather.5.cloned.1.call-done, f32[512,4096]{1,0:T(8,128)S(1)} %copy-done.1, f32[4096]{0:T(1024)S(1)} %bitcast.31, f32[512]{0:T(512)S(1)} %add_rsqrt_fusion.1, f32[512]{0:T(512)S(1)} %broadcast_multiply_fusion.1), kind=kOutput, calls=%fused_computation.45 | convolution fusion | flops 4303880192 | bytes 17846272 | tf_op jit(solution)/shard_map/dot_general | solution.py:70
  455.6 0.0 all-gather.11.cloned.1.call-update
  455.6 79.4 %all-gather.11.cloned.1.call-done = bf16[512,4096]{1,0:T(8,128)(2,1)} async-done(((bf16[512,1024]{1,0:T(8,128)(2,1)}), bf16[512,4096]{1,0:T(8,128)(2,1)}) %all-gather.11.cloned.1.call-update) | async-done | bytes 4194320 | tf_op jit(solution)/shard_map/all_gather | solution.py:50
  535.0 5.5 fusion.26
  540.5 1.0 multiply_reduce_fusion
  541.4 8.9 %select_convert_fusion = bf16[512,1024]{1,0:T(8,128)(2,1)} fusion(f32[512,4096]{1,0:T(8,128)S(1)} %get-tuple-element.5, s32[]{:T(128)S(6)} %select_n.26, bf16[4,4096,1024]{2,1,0:T(8,128)(2,1)} %all-gather.5.cloned.1.call-done, f32[4096]{0:T(1024)S(1)} %bitcast.30, f32[512]{0:T(512)S(1)} %add_rsqrt_fusion, f32[512]{0:T(512)S(1)} %broadcast_multiply_fusion, ...), kind=kOutput, calls=%fused_computation.42 | convolution fusion | flops 4305977344 | bytes 19943940 | tf_op jit(solution)/shard_map/dot_general | solution.py:70
  (25 shorter events, 0.2 us)
Async XLA Ops:
  7.2 231.5 %all-gather.5.cloned.1.call-start = ((), (), s32[]{:S(2)}) async-start(), calls=%async_computation | async-start | bytes 37748736 | tf_op jit(solution)/shard_map/all_gather | solution.py:67
  57.0 21.9 %copy-start.5 = (s32[512]{0:T(512)S(1)}, s32[512]{0:T(512)}, u32[]{:S(2)}) copy-start(s32[512]{0:T(512)} %param.11) | copy-start | bytes 6148
  77.8 253.0 %all-gather.7.cloned.1.call-start = ((), (), s32[]{:S(2)}) async-start(), calls=%async_computation.1 | async-start | bytes 5242880 | tf_op jit(solution)/shard_map/all_gather | solution.py:50
  78.0 15.6 %copy-start.3 = (bf16[512,4096]{1,0:T(8,128)(2,1)S(1)}, bf16[512,4096]{1,0:T(8,128)(2,1)}, u32[]{:S(2)}) copy-start(bf16[512,4096]{1,0:T(8,128)(2,1)} %param.9) | copy-start | bytes 12582916
  95.4 3.2 copy-start
  95.4 4.2 copy-start.4
  249.9 180.5 %all-gather.9.cloned.1.call-start = ((), (), s32[]{:S(2)}) async-start(), calls=%async_computation.2 | async-start | bytes 5242880 | tf_op jit(solution)/shard_map/all_gather | solution.py:50
  330.8 5.8 %copy-start.2 = (bf16[512,4096]{1,0:T(8,128)(2,1)S(1)}, bf16[512,4096]{1,0:T(8,128)(2,1)}, u32[]{:S(2)}) copy-start(bf16[512,4096]{1,0:T(8,128)(2,1)} %all-gather.7.cloned.1.call-done) | copy-start | bytes 12582916
  330.8 11.0 %slice-start = ((s8[8388608]{0:T(1024)(128)(4,1)}), s8[4194304]{0:T(1024)(128)(4,1)S(1)}, s32[]{:S(2)}) async-start(s8[8388608]{0:T(1024)(128)(4,1)} %bitcast.28), calls=%async_computation.4 | async-start | bytes 8388608
  336.6 5.2 slice-start.1
  351.1 183.9 %all-gather.11.cloned.1.call-start = ((), (), s32[]{:S(2)}) async-start(), calls=%async_computation.3 | async-start | bytes 5242880 | tf_op jit(solution)/shard_map/all_gather | solution.py:50
  440.7 5.8 %copy-start.1 = (f32[512,4096]{1,0:T(8,128)S(1)}, f32[512,4096]{1,0:T(8,128)}, u32[]{:S(2)}) copy-start(f32[512,4096]{1,0:T(8,128)} %get-tuple-element.7) | copy-start | bytes 25165828
Sparse Core Ops, SparseCore 0:
  77.9 160.6 all-gather.4
  250.0 80.7 all-gather.6
  351.2 79.2 all-gather.8
  455.7 79.2 all-gather.10
where the time goes:
time: 557 us
  waiting for transfers between devices  378 us (68%)
  other arithmetic  76.5 us (14%)
  blocking collectives  42.2 us (8%)
  matrix products  38.4 us (7%)
  between operations  16.1 us (3%)
    all_gather x3, waiting for transfers between devices, advance(): widened = lax.all_gather(branch, 'fsdp', axis=1, tiled=True)  239 us
    all_gather x1, waiting for transfers between devices, per_device(): gathered = lax.all_gather(weights, 'dp', axis=1, tiled=True)  139 us
    psum x1, blocking collectives, per_device(): squares = lax.psum(jnp.sum(gradients * gradients), ('dp', 'fsdp'))  42.2 us
    dot_general x4, matrix products, per_device(): jnp.dot(normed, gathered[current], preferred_element_type=jnp.float32)  38.4 us
    reduce_sum x4, other arithmetic, layer_norm(): centre = jnp.mean(stream, axis=1, keepdims=True)  23.1 us
    convert_element_type x1, other arithmetic, per_device(): weights = params_new.astype(jnp.bfloat16)  20.8 us
    sin x1, other arithmetic, position_code(): jnp.sin(across)  14.7 us
    reduce_sum x4, other arithmetic, layer_norm(): spread = jnp.mean(shifted * shifted, axis=1, keepdims=True)  11.6 us
  transfers between devices with their start and end apart: 4, of which 4 were waited for; matrix products, arithmetic and copies ran while one was open for 3% of the time, Pallas kernels for 0%

commit v1 on v0

--- a/solution.py
+++ b/solution.py
@@ -13,6 +13,16 @@
 learning_rate = 0.0024
 weight_decay = 0.05
 norm_eps = 1e-06
+
+
+def turned_line(value, axis, dim):
+    size = lax.axis_size(axis)
+    held, blocks = (value, [value])
+    for _ in range(size - 1):
+        held = lax.ppermute(held, axis, [(i, (i + 1) % size) for i in range(size)])
+        blocks.insert(0, held)
+    row_of_blocks = jnp.concatenate(blocks, axis=dim)
+    return jnp.roll(row_of_blocks, (lax.axis_index(axis) + 1) * value.shape[dim], axis=dim)
 
 
 def position_code(patch_index):
@@ -64,7 +74,7 @@
     col_first = lax.axis_index("fsdp") * col_count
     valid = lax.broadcasted_iota(jnp.int32, (tok_rows, 1), 0) < counts[0]
     stream = jnp.where(valid, tokens.astype(jnp.float32) + position_code(patch_index), 0.0)
-    gathered = lax.all_gather(weights, "dp", axis=1, tiled=True)
+    gathered = turned_line(weights, "dp", 1)
     for current in range(LAYERS):
         normed = layer_norm(stream, norm_gain[current])
         branch = jnp.dot(normed, gathered[current], preferred_element_type=jnp.float32).astype(

time: 557 us -> 802 us (1.44)
  waiting for transfers between devices: 378 us -> 564 us
  local copies, waits for them, and re-layouts: 4.64 us -> 65.8 us
    ppermute x0 -> x7, waiting for transfers between devices: none -> 324 us  [turned_line(): held = lax.ppermute(held, axis, [(i, (i + 1) % size) for i in range(size)])]
    all_gather x1 -> x0, waiting for transfers between devices: 139 us -> none  [per_device(): gathered = lax.all_gather(weights, 'dp', axis=1, tiled=True)]
    unnamed x16 -> x51, local copies, waits for them, and re-layouts: 4.59 us -> 63.2 us
  transfers between devices with their start and end apart: 4 -> 10, of which waited for: 4 -> 10; matrix products, arithmetic and copies ran while one was open for 3% -> 2% of each run, Pallas kernels for 0% -> 0%
where the time goes in v1:
time: 802 us; the launch traced here: 798 us
  waiting for transfers between devices  564 us (70%)
  other arithmetic  72.9 us (9%)
  local copies, waits for them, and re-layouts  65.8 us (8%)
  blocking collectives  42.2 us (5%)
  matrix products  36.4 us (5%)
  between operations  16.2 us (2%)
    ppermute x7, waiting for transfers between devices, turned_line(): held = lax.ppermute(held, axis, [(i, (i + 1) % size) for i in range(size)])  324 us
    all_gather x3, waiting for transfers between devices, advance(): widened = lax.all_gather(branch, 'fsdp', axis=1, tiled=True)  240 us
    unnamed x51, local copies, waits for them, and re-layouts  63.2 us
    psum x1, blocking collectives, per_device(): squares = lax.psum(jnp.sum(gradients * gradients), ('dp', 'fsdp'))  42.2 us
    dot_general x4, matrix products, per_device(): jnp.dot(normed, gathered[current], preferred_element_type=jnp.float32)  36.4 us
    reduce_sum x4, other arithmetic, layer_norm(): centre = jnp.mean(stream, axis=1, keepdims=True)  23.2 us
    convert_element_type x1, other arithmetic, per_device(): weights = params_new.astype(jnp.bfloat16)  20.8 us
  transfers between devices with their start and end apart: 10, of which 10 were waited for; matrix products, arithmetic and copies ran while one was open for 2% of the time, Pallas kernels for 0%

profile of v1, /device:TPU:0, one launch (start us, length us, event | category | flops | bytes accessed | tf_op | source)
XLA Modules:
  0.0 797.9 jit_solution(2472035535628997644)
XLA Ops:
  7.2 6.1 multiply_reduce_fusion.4
  14.0 42.2 %psum.7 = f32[]{:T(128)} all-reduce(f32[]{:T(128)} %multiply_reduce_fusion.4), channel_id=1, replica_groups=mesh['dp'=8,'fsdp'=4] {'dp','fsdp'}, use_global_device_ids=true, to_apply=%region_1.0 | all-reduce | flops 1 | bytes 8 | tf_op jit(solution)/shard_map/psum | solution.py:68
  57.0 20.8 %fusion.34 = (bf16[4,512,1024]{2,1,0:T(8,128)(2,1)}, f32[4,512,1024]{2,1,0:T(8,128)}, f32[4,512,1024]{2,1,0:T(8,128)}, f32[4,512,1024]{2,1,0:T(8,128)}) fusion(f32[4,512,1024]{2,1,0:T(8,128)} %param.14, f32[4,512,1024]{2,1,0:T(8,128)} %param.17, f32[]{:T(128)S(6)} %min.3, f32[4,512,1024]{2,1,0:T(8,128)} %param.15, f32[4,512,1024]{2,1,0:T(8,128)} %param.16), kind=kLoop, calls=%fused_computation.91 | loop fusion | flops 35651584 | bytes 62914564 | tf_op jit(solution)/shard_map/convert_element_type | solution.py:71
  77.8 49.0 %collective-permute-done = bf16[4,512,1024]{2,1,0:T(8,128)(2,1)S(1)} collective-permute-done((bf16[4,512,1024]{2,1,0:T(8,128)(2,1)}, bf16[4,512,1024]{2,1,0:T(8,128)(2,1)S(1)}, u32[]{:S(2)}, u32[]{:S(2)}) %collective-permute-start) | collective-permute-done | bytes 4194336 | tf_op jit(solution)/shard_map/ppermute | solution.py:22
  128.9 48.8 %collective-permute-done.1 = bf16[4,512,1024]{2,1,0:T(8,128)(2,1)S(1)} collective-permute-done((bf16[4,512,1024]{2,1,0:T(8,128)(2,1)S(1)}, bf16[4,512,1024]{2,1,0:T(8,128)(2,1)S(1)}, u32[]{:S(2)}, u32[]{:S(2)}) %collective-permute-start.1) | collective-permute-done | bytes 4194336 | tf_op jit(solution)/shard_map/ppermute | solution.py:22
  179.7 48.8 %collective-permute-done.2 = bf16[4,512,1024]{2,1,0:T(8,128)(2,1)S(1)} collective-permute-done((bf16[4,512,1024]{2,1,0:T(8,128)(2,1)S(1)}, bf16[4,512,1024]{2,1,0:T(8,128)(2,1)S(1)}, u32[]{:S(2)}, u32[]{:S(2)}) %collective-permute-start.2) | collective-permute-done | bytes 4194336 | tf_op jit(solution)/shard_map/ppermute | solution.py:22
  230.4 48.8 %collective-permute-done.3 = bf16[4,512,1024]{2,1,0:T(8,128)(2,1)S(1)} collective-permute-done((bf16[4,512,1024]{2,1,0:T(8,128)(2,1)S(1)}, bf16[4,512,1024]{2,1,0:T(8,128)(2,1)S(1)}, u32[]{:S(2)}, u32[]{:S(2)}) %collective-permute-start.3) | collective-permute-done | bytes 4194336 | tf_op jit(solution)/shard_map/ppermute | solution.py:22
  281.3 48.8 %collective-permute-done.4 = bf16[4,512,1024]{2,1,0:T(8,128)(2,1)S(1)} collective-permute-done((bf16[4,512,1024]{2,1,0:T(8,128)(2,1)S(1)}, bf16[4,512,1024]{2,1,0:T(8,128)(2,1)S(1)}, u32[]{:S(2)}, u32[]{:S(2)}) %collective-permute-start.4) | collective-permute-done | bytes 4194336 | tf_op jit(solution)/shard_map/ppermute | solution.py:22
  332.2 48.9 %collective-permute-done.5 = bf16[4,512,1024]{2,1,0:T(8,128)(2,1)} collective-permute-done((bf16[4,512,1024]{2,1,0:T(8,128)(2,1)S(1)}, bf16[4,512,1024]{2,1,0:T(8,128)(2,1)}, u32[]{:S(2)}, u32[]{:S(2)}) %collective-permute-start.5) | collective-permute-done | bytes 4194336 | tf_op jit(solution)/shard_map/ppermute | solution.py:22
  382.3 14.7 %multiply_sine_fusion.1 = (f32[512,1024]{1,0:T(8,128)S(1)}, f32[512,1024]{1,0:T(8,128)S(1)}, f32[512,1024]{1,0:T(8,128)S(1)}, f32[512,1024]{1,0:T(8,128)S(1)}) fusion(f32[1024]{0:T(1024)S(1)} %negate_power_fusion, f32[512]{0:T(512)S(1)} %get-tuple-element.24, f32[512]{0:T(512)S(1)} %get-tuple-element.25), kind=kLoop, calls=%fused_computation.41 | loop fusion | flops 1048576 | bytes 8396800 | tf_op jit(solution)/shard_map/sin | solution.py:34
  399.8 30.9 %collective-permute-done.6 = bf16[4,512,1024]{2,1,0:T(8,128)(2,1)} collective-permute-done((bf16[4,512,1024]{2,1,0:T(8,128)(2,1)}, bf16[4,512,1024]{2,1,0:T(8,128)(2,1)}, u32[]{:S(2)}, u32[]{:S(2)}) %collective-permute-start.6) | collective-permute-done | bytes 4194336 | tf_op jit(solution)/shard_map/ppermute | solution.py:22
  430.7 4.7 constant_dynamic-update-slice_fusion.15
  435.3 4.9 constant_dynamic-update-slice_fusion.14
  440.3 2.6 constant_dynamic-update-slice_fusion.13
  442.9 2.7 constant_dynamic-update-slice_fusion.12
  445.6 2.6 constant_dynamic-update-slice_fusion.11
  448.2 2.6 constant_dynamic-update-slice_fusion.10
  455.8 4.8 constant_dynamic-update-slice_fusion.7
  460.6 4.8 constant_dynamic-update-slice_fusion.6
  465.3 4.7 constant_dynamic-update-slice_fusion.5
  472.5 2.6 constant_dynamic-update-slice_fusion.3
  482.7 9.3 %fusion.18 = bf16[512,1024]{1,0:T(8,128)(2,1)} fusion(bf16[4,8192,1024]{2,1,0:T(8,128)(2,1)} %constant_dynamic-update-slice_fusion, s32[]{:T(128)S(6)} %select_n.39, f32[512,4096]{1,0:T(8,128)S(1)} %get-tuple-element.9, f32[4096]{0:T(1024)S(1)} %bitcast.31, f32[512]{0:T(512)S(1)} %add_rsqrt_fusion.3, f32[512]{0:T(512)S(1)} %broadcast_multiply_fusion.3), kind=kOutput, calls=%fused_computation.43 | convolution fusion | flops 4303880192 | bytes 17846276 | tf_op jit(solution)/shard_map/dot_general | solution.py:80
  492.0 80.8 %all-gather.4.cloned.1.call-done = bf16[512,4096]{1,0:T(8,128)(2,1)} async-done(((bf16[512,1024]{1,0:T(8,128)(2,1)}), bf16[512,4096]{1,0:T(8,128)(2,1)}) %all-gather.4.cloned.1.call-update) | async-done | bytes 4194320 | tf_op jit(solution)/shard_map/all_gather | solution.py:60
  572.9 5.6 fusion.22
  582.5 9.2 %fusion.19 = bf16[512,1024]{1,0:T(8,128)(2,1)} fusion(bf16[4,8192,1024]{2,1,0:T(8,128)(2,1)} %constant_dynamic-update-slice_fusion, s32[]{:T(128)S(6)} %add.110, s32[]{:T(128)S(6)} %select_n.39, f32[4096]{0:T(1024)S(1)} %bitcast.30, f32[512]{0:T(512)S(1)} %add_rsqrt_fusion.2, f32[512]{0:T(512)S(1)} %broadcast_multiply_fusion.2, ...), kind=kOutput, calls=%fused_computation.44 | convolution fusion | flops 4308074496 | bytes 22040584 | tf_op jit(solution)/shard_map/dot_general | solution.py:80
  591.8 79.3 %all-gather.6.cloned.1.call-done = bf16[512,4096]{1,0:T(8,128)(2,1)} async-done(((bf16[512,1024]{1,0:T(8,128)(2,1)}), bf16[512,4096]{1,0:T(8,128)(2,1)}) %all-gather.6.cloned.1.call-update) | async-done | bytes 4194320 | tf_op jit(solution)/shard_map/all_gather | solution.py:60
  671.1 10.4 %fusion.31 = (f32[512]{0:T(512)S(1)}, f32[512,4096]{1,0:T(8,128)}) fusion(bf16[512,4096]{1,0:T(8,128)(2,1)} %all-gather.6.cloned.1.call-done, f32[512,4096]{1,0:T(8,128)} %copy-done, bf16[512,4096]{1,0:T(8,128)(2,1)} %all-gather.4.cloned.1.call-done), kind=kLoop, calls=%fused_computation.89 | loop fusion | flops 10485248 | bytes 25167872 | tf_op jit(solution)/shard_map/reduce_sum | solution.py:39
  681.5 4.5 multiply_reduce_fusion.1
  687.3 9.0 %fusion.20 = bf16[512,1024]{1,0:T(8,128)(2,1)} fusion(bf16[4,8192,1024]{2,1,0:T(8,128)(2,1)} %constant_dynamic-update-slice_fusion, s32[]{:T(128)S(6)} %add.111, s32[]{:T(128)S(6)} %select_n.39, f32[512,4096]{1,0:T(8,128)S(1)} %copy-done.2, f32[4096]{0:T(1024)S(1)} %bitcast.29, f32[512]{0:T(512)S(1)} %add_rsqrt_fusion.1, f32[512]{0:T(512)S(1)} %broadcast_multiply_fusion.1), kind=kOutput, calls=%fused_computation.45 | convolution fusion | flops 4303880192 | bytes 17846280 | tf_op jit(solution)/shard_map/dot_general | solution.py:80
  696.4 79.4 %all-gather.8.cloned.1.call-done = bf16[512,4096]{1,0:T(8,128)(2,1)} async-done(((bf16[512,1024]{1,0:T(8,128)(2,1)}), bf16[512,4096]{1,0:T(8,128)(2,1)}) %all-gather.8.cloned.1.call-update) | async-done | bytes 4194320 | tf_op jit(solution)/shard_map/all_gather | solution.py:60
  775.8 5.5 fusion.30
  782.2 8.9 %select_convert_fusion = bf16[512,1024]{1,0:T(8,128)(2,1)} fusion(f32[512,4096]{1,0:T(8,128)S(1)} %get-tuple-element.5, s32[]{:T(128)S(6)} %select_n.40, bf16[4,8192,1024]{2,1,0:T(8,128)(2,1)} %constant_dynamic-update-slice_fusion, s32[]{:T(128)S(6)} %add.112, s32[]{:T(128)S(6)} %select_n.39, f32[4096]{0:T(1024)S(1)} %bitcast.28, ...), kind=kOutput, calls=%fused_computation.42 | convolution fusion | flops 4305977344 | bytes 19943948 | tf_op jit(solution)/shard_map/dot_general | solution.py:80
  (71 shorter events, 34.7 us)
Async XLA Ops:
  7.2 565.7 %all-gather.4.cloned.1.call-start = ((), (), s32[]{:S(2)}) async-start(), calls=%async_computation | async-start | bytes 5242880 | tf_op jit(solution)/shard_map/all_gather | solution.py:60
  57.0 325.3 %copy-start.17 = (s32[512]{0:T(512)S(1)}, s32[512]{0:T(512)}, u32[]{:S(2)}) copy-start(s32[512]{0:T(512)} %param.11) | copy-start | bytes 6148
  77.8 49.0 %collective-permute-start = (bf16[4,512,1024]{2,1,0:T(8,128)(2,1)}, bf16[4,512,1024]{2,1,0:T(8,128)(2,1)S(1)}, u32[]{:S(2)}, u32[]{:S(2)}) collective-permute-start(bf16[4,512,1024]{2,1,0:T(8,128)(2,1)} %get-tuple-element.10), channel_id=1, source_target_pairs={{0,4},{4,8},{8,12},{12,16},{16,20},{20,24},{24,28},{28,0},{1,5},{5... | collective-permute-start | bytes 12582920 | tf_op jit(solution)/shard_map/ppermute | solution.py:22
  126.9 2.0 copy-start.5
  128.8 48.8 %collective-permute-start.1 = (bf16[4,512,1024]{2,1,0:T(8,128)(2,1)S(1)}, bf16[4,512,1024]{2,1,0:T(8,128)(2,1)S(1)}, u32[]{:S(2)}, u32[]{:S(2)}) collective-permute-start(bf16[4,512,1024]{2,1,0:T(8,128)(2,1)S(1)} %collective-permute-done), channel_id=1, source_target_pairs={{0,4},{4,8},{8,12},{12,16},{16,20},{20,24},{24,28},{28,0},{1,5},{5... | collective-permute-start | bytes 12582920 | tf_op jit(solution)/shard_map/ppermute | solution.py:22
  177.7 2.0 copy-start.7
  179.7 48.8 %collective-permute-start.2 = (bf16[4,512,1024]{2,1,0:T(8,128)(2,1)S(1)}, bf16[4,512,1024]{2,1,0:T(8,128)(2,1)S(1)}, u32[]{:S(2)}, u32[]{:S(2)}) collective-permute-start(bf16[4,512,1024]{2,1,0:T(8,128)(2,1)S(1)} %collective-permute-done.1), channel_id=1, source_target_pairs={{0,4},{4,8},{8,12},{12,16},{16,20},{20,24},{24,28},{28,0},{1,5},{5... | collective-permute-start | bytes 12582920 | tf_op jit(solution)/shard_map/ppermute | solution.py:22
  228.5 2.0 copy-start.9
  230.4 48.8 %collective-permute-start.3 = (bf16[4,512,1024]{2,1,0:T(8,128)(2,1)S(1)}, bf16[4,512,1024]{2,1,0:T(8,128)(2,1)S(1)}, u32[]{:S(2)}, u32[]{:S(2)}) collective-permute-start(bf16[4,512,1024]{2,1,0:T(8,128)(2,1)S(1)} %collective-permute-done.2), channel_id=1, source_target_pairs={{0,4},{4,8},{8,12},{12,16},{16,20},{20,24},{24,28},{28,0},{1,5},{5... | collective-permute-start | bytes 12582920 | tf_op jit(solution)/shard_map/ppermute | solution.py:22
  279.3 2.1 copy-start.11
  281.3 48.8 %collective-permute-start.4 = (bf16[4,512,1024]{2,1,0:T(8,128)(2,1)S(1)}, bf16[4,512,1024]{2,1,0:T(8,128)(2,1)S(1)}, u32[]{:S(2)}, u32[]{:S(2)}) collective-permute-start(bf16[4,512,1024]{2,1,0:T(8,128)(2,1)S(1)} %collective-permute-done.3), channel_id=1, source_target_pairs={{0,4},{4,8},{8,12},{12,16},{16,20},{20,24},{24,28},{28,0},{1,5},{5... | collective-permute-start | bytes 12582920 | tf_op jit(solution)/shard_map/ppermute | solution.py:22
  330.2 2.0 copy-start.13
  332.2 48.9 %collective-permute-start.5 = (bf16[4,512,1024]{2,1,0:T(8,128)(2,1)S(1)}, bf16[4,512,1024]{2,1,0:T(8,128)(2,1)}, u32[]{:S(2)}, u32[]{:S(2)}) collective-permute-start(bf16[4,512,1024]{2,1,0:T(8,128)(2,1)S(1)} %collective-permute-done.4), channel_id=1, source_target_pairs={{0,4},{4,8},{8,12},{12,16},{16,20},{20,24},{24,28},{28,0},{1,5},{5... | collective-permute-start | bytes 12582920 | tf_op jit(solution)/shard_map/ppermute | solution.py:22
  381.1 49.6 %collective-permute-start.6 = (bf16[4,512,1024]{2,1,0:T(8,128)(2,1)}, bf16[4,512,1024]{2,1,0:T(8,128)(2,1)}, u32[]{:S(2)}, u32[]{:S(2)}) collective-permute-start(bf16[4,512,1024]{2,1,0:T(8,128)(2,1)} %collective-permute-done.5), channel_id=1, source_target_pairs={{0,4},{4,8},{8,12},{12,16},{16,20},{20,24},{24,28},{28,0},{1,5},{5... | collective-permute-start | bytes 12582920 | tf_op jit(solution)/shard_map/ppermute | solution.py:22
  382.2 14.8 %copy-start.15 = (bf16[512,4096]{1,0:T(8,128)(2,1)S(1)}, bf16[512,4096]{1,0:T(8,128)(2,1)}, u32[]{:S(2)}) copy-start(bf16[512,4096]{1,0:T(8,128)(2,1)} %param.9) | copy-start | bytes 12582916
  398.7 84.0 %copy-start = (f32[512,4096]{1,0:T(8,128)}, f32[512,4096]{1,0:T(8,128)S(1)}, u32[]{:S(2)}) copy-start(f32[512,4096]{1,0:T(8,128)S(1)} %get-tuple-element.9) | copy-start | bytes 25165828
  398.7 1.0 copy-start.16
  399.8 40.5 %copy-start.14 = (bf16[4,512,1024]{2,1,0:T(8,128)(2,1)S(1)}, bf16[4,512,1024]{2,1,0:T(8,128)(2,1)}, u32[]{:S(2)}) copy-start(bf16[4,512,1024]{2,1,0:T(8,128)(2,1)} %copy-done.13) | copy-start | bytes 12582916
  435.3 7.5 copy-start.12
  440.3 5.3 copy-start.10
  442.9 5.3 copy-start.8
  445.6 5.2 copy-start.6
  448.2 5.1 copy-start.3
  492.0 179.1 %all-gather.6.cloned.1.call-start = ((), (), s32[]{:S(2)}) async-start(), calls=%async_computation.1 | async-start | bytes 5242880 | tf_op jit(solution)/shard_map/all_gather | solution.py:60
  572.9 7.0 copy-start.1
  572.9 8.2 %copy-start.4 = (bf16[512,4096]{1,0:T(8,128)(2,1)S(1)}, bf16[512,4096]{1,0:T(8,128)(2,1)}, u32[]{:S(2)}) copy-start(bf16[512,4096]{1,0:T(8,128)(2,1)} %all-gather.4.cloned.1.call-done) | copy-start | bytes 12582916
  591.7 184.0 %all-gather.8.cloned.1.call-start = ((), (), s32[]{:S(2)}) async-start(), calls=%async_computation.2 | async-start | bytes 5242880 | tf_op jit(solution)/shard_map/all_gather | solution.py:60
  681.5 5.8 copy-start.2
Sparse Core Ops, SparseCore 0:
  492.1 80.7 all-gather.3
  591.9 79.2 all-gather.5
  696.5 79.2 all-gather.7
